TPU v7x, 32 devices: a whole 2x2x4 slice. The times are simulated.
32 devices in a mesh: dom: 32 (over z, y, x, core).
Axes of the slice: x: 2, y: 2, z: 4, core: 2. Of those that a mesh axis runs over, the one named last changes fastest.
Arguments:
- node_emb: bfloat16 [16384, 64], P('dom'), may hold values from -6 to 6
- hub_emb: bfloat16 [256, 64], replicated, may hold values from -6 to 6
- tile_vals: bfloat16 [4096, 128, 128], P('dom')
- tile_col: int32 [4096], P('dom'), may hold values from 0 to 5
- tile_dest: int32 [4096], P('dom'), may hold values from 0 to 29, as said below
Outputs:
- node_out: float32 [16384, 64], P('dom')
- hub_out: float32 [256, 64], replicated
Inputs may be any that keep to these rules, and one draw needn't show every extreme that they name: tile_dest below 28 names a partition offset from -3 to 3 and a block of that partition; from 28 up it names a hub block. tile_col below 4 names one of the holding partition's own blocks; from 4 up it names a hub block.
All inputs are finite; a program needn't handle non-finite values.
Results may differ from a plain program's by a relative error of at most 0.0003.
Values sent between devices are 32-bit elements.
A program may use at most 64 MiB of HBM per device.

v0:
```python
import jax
import jax.numpy as jnp
from jax import lax
from jax.sharding import PartitionSpec as P

REACH_BITS = 2
LAYERS = 2


def shifted(block, axis, distance):
    devices = range(lax.axis_size(axis))
    route = [((i - distance) % len(devices), i) for i in devices]
    return lax.ppermute(block, axis, route)


def route_partials(spread, farthest):
    overall = spread[farthest]
    for heading in (1, -1):
        for distance in range(1, farthest + 1):
            overall = overall + shifted(
                spread[farthest + heading * distance], "dom", heading * distance
            )
    return overall


def shards(node_emb, hub_emb, tile_vals, tile_col, tile_dest):
    tile_size = tile_vals.shape[1]
    features = node_emb.shape[1]
    dev_rows = node_emb.shape[0]
    own_blocks = dev_rows // tile_size
    hub_rows = hub_emb.shape[0]
    hub_blocks = hub_rows // tile_size
    tile_count = tile_vals.shape[0]
    farthest = 2**REACH_BITS - 1
    slot_count = 2 * farthest + 1
    target_count = slot_count * own_blocks + hub_blocks
    one_hot = (tile_dest[None, :] == jnp.arange(target_count, dtype=jnp.int32)[:, None]).astype(
        jnp.float32
    )
    current_node = node_emb
    current_hub = hub_emb
    node_total = node_emb.astype(jnp.float32)
    hub_total = hub_emb.astype(jnp.float32)
    for layer_index in range(LAYERS):
        sources = jnp.concatenate([current_node, current_hub], 0).reshape(
            own_blocks + hub_blocks, tile_size, features
        )
        picked = jnp.take(sources, tile_col, axis=0)
        products = jnp.einsum("tij,tjd->tid", tile_vals, picked, preferred_element_type=jnp.float32)
        summed = jnp.dot(
            one_hot,
            products.reshape(tile_count, tile_size * features),
            precision=lax.Precision.HIGHEST,
            preferred_element_type=jnp.float32,
        )
        spread = summed[: slot_count * own_blocks].reshape(slot_count, dev_rows, features)
        hub_part = summed[slot_count * own_blocks :].reshape(hub_rows, features)
        hub_sum = lax.psum(hub_part, "dom")
        node_sum = route_partials(spread, farthest)
        node_total = node_total + node_sum
        hub_total = hub_total + hub_sum
        current_node = node_sum.astype(jnp.bfloat16)
        current_hub = hub_sum.astype(jnp.bfloat16)
    return (node_total / float(LAYERS + 1), hub_total / float(LAYERS + 1))


def solution(mesh):
    in_specs = (P("dom", None), P(), P("dom", None, None), P("dom"), P("dom"))
    out_specs = (P("dom", None), P())
    return jax.shard_map(shards, mesh=mesh, in_specs=in_specs, out_specs=out_specs, check_vma=False)
```

profile of v0, /device:TPU:0, one launch (start us, length us, event | category | flops | bytes accessed | tf_op | source)
XLA Modules:
  0.0 341.6 jit_solution(637796549837110401)
XLA Ops:
  7.2 0.0 all-reduce.3.cloned.1.call-start
  7.2 0.7 compare_select_fusion
  7.9 0.7 compare_and_fusion
  8.5 0.9 copy_bitcast_fusion
  9.4 1.0 gather_fusion
  10.4 7.1 %convolution_bitcast_fusion.1 = f32[128,128,64]{1,2,0:T(8,128)} fusion(bf16[128,128,128]{2,1,0:T(8,128)(2,1)} %param.9, bf16[128,128,64]{1,2,0:T(8,128)(2,1)S(1)} %gather_fusion, pred[128]{0:T(512)(128)(4,1)S(1)} %compare_and_fusion), kind=kOutput, calls=%fused_computation.3 | convolution fusion | flops 269484032 | bytes 10485888 | tf_op jit(solution)/shard_map/tij,tjd->tid/dot_general | solution.py:49
  17.5 5.5 %copy.25 = f32[128,128,64]{0,2,1:T(8,128)} copy(f32[128,128,64]{1,2,0:T(8,128)} %convolution_bitcast_fusion.1) | data formatting | bytes 8388608 | tf_op jit(solution)/shard_map/tij,tjd->tid/dot_general | solution.py:49
  22.9 4.6 %fusion.7 = f32[30,8192]{1,0:T(8,128)S(1)} fusion(f32[128,8192]{0,1:T(8,128)} %bitcast.16, s32[128]{0:T(128)S(1)} %copy-done.3), kind=kOutput, calls=%fused_computation.18 | convolution fusion | flops 377491200 | bytes 5177856 | tf_op jit(solution)/shard_map/dot_general | solution.py:50
  27.5 0.1 fusion.14
  27.7 0.2 squeeze.43
  27.8 0.5 collective-permute-start
  28.4 0.2 squeeze.44
  28.6 2.5 collective-permute-start.1
  31.1 0.2 squeeze.45
  31.3 2.4 collective-permute-start.2
  33.7 0.9 squeeze.46
  34.6 3.0 collective-permute-start.3
  37.6 0.9 squeeze.47
  38.4 1.2 collective-permute-start.4
  39.6 0.9 squeeze.48
  40.5 0.2 collective-permute-done
  40.7 0.3 collective-permute-start.5
  41.0 0.8 reshape.60
  41.8 0.0 all-reduce.3.cloned.1.call-update
  41.8 0.2 all-reduce.5.cloned.1.call-start
  42.1 0.2 squeeze.42
  42.3 134.6 %all-reduce.3.cloned.1.call-done = f32[256,64]{1,0:T(8,128)} async-done(((f32[256,64]{1,0:T(8,128)}), f32[256,64]{1,0:T(8,128)}) %all-reduce.3.cloned.1.call-update) | async-done | bytes 65552 | tf_op jit(solution)/shard_map/psum | solution.py:58
  176.8 0.9 convert_element_type.15
  177.7 0.0 collective-permute-done.1
  177.8 0.0 collective-permute-done.3
  177.8 0.0 collective-permute-done.4
  177.8 0.1 fusion.12
  177.9 0.1 copy.27
  178.1 1.0 gather_fusion.1
  179.0 7.1 %convolution_bitcast_fusion = f32[128,128,64]{1,2,0:T(8,128)} fusion(bf16[128,128,128]{2,1,0:T(8,128)(2,1)} %param.9, bf16[128,128,64]{1,2,0:T(8,128)(2,1)S(1)} %gather_fusion.1, pred[128]{0:T(512)(128)(4,1)S(1)} %compare_and_fusion), kind=kOutput, calls=%fused_computation.2 | convolution fusion | flops 269484032 | bytes 10485888 | tf_op jit(solution)/shard_map/tij,tjd->tid/dot_general | solution.py:49
  186.1 5.4 %copy.28 = f32[128,128,64]{0,2,1:T(8,128)} copy(f32[128,128,64]{1,2,0:T(8,128)} %convolution_bitcast_fusion) | data formatting | bytes 8388608 | tf_op jit(solution)/shard_map/tij,tjd->tid/dot_general | solution.py:49
  191.6 4.6 %fusion.6 = f32[30,8192]{1,0:T(8,128)S(1)} fusion(f32[128,8192]{0,1:T(8,128)} %bitcast.17, s32[128]{0:T(128)S(1)} %copy-done.3), kind=kOutput, calls=%fused_computation.17 | convolution fusion | flops 377491200 | bytes 5177856 | tf_op jit(solution)/shard_map/dot_general | solution.py:50
  196.2 0.1 fusion.13
  196.3 0.2 squeeze.54
  196.5 3.3 collective-permute-start.10
  199.9 0.8 reshape.63
  200.7 0.0 all-reduce.5.cloned.1.call-update
  200.7 0.1 copy.23
  200.8 0.1 copy.29
  200.9 0.2 squeeze.55
  201.1 0.0 collective-permute-start.11
  201.2 0.9 squeeze.50
  202.1 1.6 collective-permute-start.6
  203.6 0.9 squeeze.51
  204.5 0.6 collective-permute-start.7
  205.1 0.9 squeeze.52
  206.0 0.0 collective-permute-start.8
  206.0 0.9 squeeze.53
  206.8 0.2 squeeze.49
  207.0 2.2 collective-permute-done.10
  209.2 2.2 collective-permute-start.9
  211.5 120.8 %all-reduce.5.cloned.1.call-done = f32[256,64]{1,0:T(8,128)} async-done(((f32[256,64]{1,0:T(8,128)}), f32[256,64]{1,0:T(8,128)}) %all-reduce.5.cloned.1.call-update) | async-done | bytes 65552 | tf_op jit(solution)/shard_map/psum | solution.py:58
  332.2 0.9 add_multiply_fusion.1
  333.2 0.7 copy.31
  333.9 0.0 collective-permute-done.7
  333.9 0.0 collective-permute-done.8
  333.9 0.0 collective-permute-done.9
  333.9 0.1 add_multiply_fusion
  334.0 0.8 copy.30
  (16 shorter events, 0.1 us)
Async XLA Ops:
  7.2 169.7 %all-reduce.3.cloned.1.call-start = ((), (), s32[]{:S(2)}) async-start(), calls=%async_computation | async-start | bytes 262144 | tf_op jit(solution)/shard_map/psum | solution.py:58
  17.5 5.5 %copy-start.3 = (s32[128]{0:T(128)S(1)}, s32[128]{0:T(128)}, u32[]{:S(2)}) copy-start(s32[128]{0:T(128)} %param.11) | copy-start | bytes 1540
  27.8 12.9 %collective-permute-start = (f32[512,64]{1,0:T(8,128)S(1)}, f32[512,64]{1,0:T(8,128)S(1)}, u32[]{:S(2)}, u32[]{:S(2)}) collective-permute-start(f32[512,64]{1,0:T(8,128)S(1)} %squeeze.43), channel_id=1, source_target_pairs={{31,0},{0,1},{1,2},{2,3},{3,4},{4,5},{5,6},{6,7},{7,8},{8,9},{9,10... | collective-permute-start | bytes 393224 | tf_op jit(solution)/shard_map/ppermute | solution.py:13
  28.6 149.2 %collective-permute-start.1 = (f32[512,64]{1,0:T(8,128)S(1)}, f32[512,64]{1,0:T(8,128)S(1)}, u32[]{:S(2)}, u32[]{:S(2)}) collective-permute-start(f32[512,64]{1,0:T(8,128)S(1)} %squeeze.44), channel_id=1, source_target_pairs={{30,0},{31,1},{0,2},{1,3},{2,4},{3,5},{4,6},{5,7},{6,8},{7,9},{8,1... | collective-permute-start | bytes 393224 | tf_op jit(solution)/shard_map/ppermute | solution.py:13
  31.3 146.5 %collective-permute-start.2 = (f32[512,64]{1,0:T(8,128)S(1)}, f32[512,64]{1,0:T(8,128)S(1)}, u32[]{:S(2)}, u32[]{:S(2)}) collective-permute-start(f32[512,64]{1,0:T(8,128)S(1)} %squeeze.45), channel_id=1, source_target_pairs={{29,0},{30,1},{31,2},{0,3},{1,4},{2,5},{3,6},{4,7},{5,8},{6,9},{7,... | collective-permute-start | bytes 393224 | tf_op jit(solution)/shard_map/ppermute | solution.py:13
  34.6 143.2 %collective-permute-start.3 = (f32[512,64]{1,0:T(8,128)}, f32[512,64]{1,0:T(8,128)S(1)}, u32[]{:S(2)}, u32[]{:S(2)}) collective-permute-start(f32[512,64]{1,0:T(8,128)} %squeeze.46), channel_id=1, source_target_pairs={{1,0},{2,1},{3,2},{4,3},{5,4},{6,5},{7,6},{8,7},{9,8},{10,9},{11,1... | collective-permute-start | bytes 393224 | tf_op jit(solution)/shard_map/ppermute | solution.py:13
  38.4 139.3 %collective-permute-start.4 = (f32[512,64]{1,0:T(8,128)}, f32[512,64]{1,0:T(8,128)S(1)}, u32[]{:S(2)}, u32[]{:S(2)}) collective-permute-start(f32[512,64]{1,0:T(8,128)} %squeeze.47), channel_id=1, source_target_pairs={{2,0},{3,1},{4,2},{5,3},{6,4},{7,5},{8,6},{9,7},{10,8},{11,9},{12,... | collective-permute-start | bytes 393224 | tf_op jit(solution)/shard_map/ppermute | solution.py:13
  40.7 137.1 %collective-permute-start.5 = (f32[512,64]{1,0:T(8,128)}, f32[512,64]{1,0:T(8,128)S(1)}, u32[]{:S(2)}, u32[]{:S(2)}) collective-permute-start(f32[512,64]{1,0:T(8,128)} %squeeze.48), channel_id=1, source_target_pairs={{3,0},{4,1},{5,2},{6,3},{7,4},{8,5},{9,6},{10,7},{11,8},{12,9},{13... | collective-permute-start | bytes 393224 | tf_op jit(solution)/shard_map/ppermute | solution.py:13
  41.8 290.4 %all-reduce.5.cloned.1.call-start = ((), (), s32[]{:S(2)}) async-start(), calls=%async_computation.1 | async-start | bytes 262144 | tf_op jit(solution)/shard_map/psum | solution.py:58
  191.6 9.1 %copy-start.1 = (bf16[512,64]{0,1:T(8,128)(2,1)S(1)}, bf16[512,64]{0,1:T(8,128)(2,1)}, u32[]{:S(2)}) copy-start(bf16[512,64]{0,1:T(8,128)(2,1)} %param.7) | copy-start | bytes 196612
  191.6 9.2 %copy-start.2 = (bf16[256,64]{0,1:T(8,128)(2,1)S(1)}, bf16[256,64]{0,1:T(8,128)(2,1)}, u32[]{:S(2)}) copy-start(bf16[256,64]{0,1:T(8,128)(2,1)} %param.8) | copy-start | bytes 98308
  191.6 140.6 %copy-start = (f32[256,64]{1,0:T(8,128)S(1)}, f32[256,64]{1,0:T(8,128)}, u32[]{:S(2)}) copy-start(f32[256,64]{1,0:T(8,128)} %all-reduce.3.cloned.1.call-done) | copy-start | bytes 196612
  196.5 12.7 %collective-permute-start.10 = (f32[512,64]{1,0:T(8,128)S(1)}, f32[512,64]{1,0:T(8,128)S(1)}, u32[]{:S(2)}, u32[]{:S(2)}) collective-permute-start(f32[512,64]{1,0:T(8,128)S(1)} %squeeze.54), channel_id=1, source_target_pairs={{2,0},{3,1},{4,2},{5,3},{6,4},{7,5},{8,6},{9,7},{10,8},{11,9},{12,... | collective-permute-start | bytes 393224 | tf_op jit(solution)/shard_map/ppermute | solution.py:13
  201.1 132.7 %collective-permute-start.11 = (f32[512,64]{1,0:T(8,128)S(1)}, f32[512,64]{1,0:T(8,128)S(1)}, u32[]{:S(2)}, u32[]{:S(2)}) collective-permute-start(f32[512,64]{1,0:T(8,128)S(1)} %squeeze.55), channel_id=1, source_target_pairs={{3,0},{4,1},{5,2},{6,3},{7,4},{8,5},{9,6},{10,7},{11,8},{12,9},{13... | collective-permute-start | bytes 393224 | tf_op jit(solution)/shard_map/ppermute | solution.py:13
  202.1 131.8 %collective-permute-start.6 = (f32[512,64]{1,0:T(8,128)}, f32[512,64]{1,0:T(8,128)S(1)}, u32[]{:S(2)}, u32[]{:S(2)}) collective-permute-start(f32[512,64]{1,0:T(8,128)} %squeeze.50), channel_id=1, source_target_pairs={{31,0},{0,1},{1,2},{2,3},{3,4},{4,5},{5,6},{6,7},{7,8},{8,9},{9,10... | collective-permute-start | bytes 393224 | tf_op jit(solution)/shard_map/ppermute | solution.py:13
  204.5 129.4 %collective-permute-start.7 = (f32[512,64]{1,0:T(8,128)}, f32[512,64]{1,0:T(8,128)S(1)}, u32[]{:S(2)}, u32[]{:S(2)}) collective-permute-start(f32[512,64]{1,0:T(8,128)} %squeeze.51), channel_id=1, source_target_pairs={{30,0},{31,1},{0,2},{1,3},{2,4},{3,5},{4,6},{5,7},{6,8},{7,9},{8,1... | collective-permute-start | bytes 393224 | tf_op jit(solution)/shard_map/ppermute | solution.py:13
  206.0 127.9 %collective-permute-start.8 = (f32[512,64]{1,0:T(8,128)}, f32[512,64]{1,0:T(8,128)S(1)}, u32[]{:S(2)}, u32[]{:S(2)}) collective-permute-start(f32[512,64]{1,0:T(8,128)} %squeeze.52), channel_id=1, source_target_pairs={{29,0},{30,1},{31,2},{0,3},{1,4},{2,5},{3,6},{4,7},{5,8},{6,9},{7,... | collective-permute-start | bytes 393224 | tf_op jit(solution)/shard_map/ppermute | solution.py:13
  209.2 124.7 %collective-permute-start.9 = (f32[512,64]{1,0:T(8,128)}, f32[512,64]{1,0:T(8,128)S(1)}, u32[]{:S(2)}, u32[]{:S(2)}) collective-permute-start(f32[512,64]{1,0:T(8,128)} %squeeze.53), channel_id=1, source_target_pairs={{1,0},{2,1},{3,2},{4,3},{5,4},{6,5},{7,6},{8,7},{9,8},{10,9},{11,1... | collective-permute-start | bytes 393224 | tf_op jit(solution)/shard_map/ppermute | solution.py:13
Sparse Core Ops, SparseCore 0:
  42.0 134.8 all-reduce.2
  200.8 131.3 all-reduce.4
where the time goes:
time: 342 us
  waiting for transfers between devices  258 us (75%)
  local copies, waits for them, and re-layouts  24.1 us (7%)
  matrix products  23.3 us (7%)
  starting transfers between devices  17.9 us (5%)
  between operations  14.2 us (4%)
  other arithmetic  4.29 us (1%)
    psum x2, waiting for transfers between devices, shards(): hub_sum = lax.psum(hub_part, 'dom')  255 us
    ppermute x12, starting transfers between devices, shifted(): return lax.ppermute(block, axis, route)  17.6 us
    dot_general x2, matrix products, shards(): jnp.einsum('tij,tjd->tid', tile_vals, picked, preferred_element_type=jnp....  14.1 us
    dot_general x2, local copies, waits for them, and re-layouts, shards(): jnp.einsum('tij,tjd->tid', tile_vals, picked, preferred_element_type=jnp....  10.9 us
    dot_general x2, matrix products, shards(): jnp.dot(one_hot, products.reshape(tile_count, tile_size * features), prec...  9.19 us
    squeeze x12, local copies, waits for them, and re-layouts, route_partials(): spread[farthest + heading * distance]  7.08 us
  transfers between devices with their start and end apart: 14, of which 4 were waited for; matrix products, arithmetic and copies ran while one was open for 3% of the time, Pallas kernels for 0%

commit v1 on v0

v1 whole, which is shorter than its diff:
```python
import functools
import jax
import jax.numpy as jnp
from jax import lax
from jax.experimental import pallas as pl
from jax.experimental.pallas import tpu as pltpu
from jax.sharding import PartitionSpec as P

REACH_BITS = 2
LAYERS = 2
CHUNKS = 8
GROUP = 4
SUBLANES = 8
MESH = pl.DeviceIdType.MESH


def kernel(
    n, pieces, vals_hbm, col_ref, prev_ref, last_ref, node_ref, hub_ref,
    node_out, hub_out,
    vals, cur, chain, own, hub_own, pair, hub_pair, merged, arrived,
    hub_half, hub_got, hub_all, node_total, hub_total,
    load_sem, pair_send, pair_recv, node_send, node_recv, hub_pair_sem,
    piece_send, piece_recv, cast_send, cast_recv,
):
    me = lax.axis_index("dom")
    parity = lax.rem(me, 2)
    chip = me // 2
    chips = n // 2
    step = 1 - 2 * parity
    partner = me + step
    tiles, tile, _ = vals.shape
    width = node_ref.shape[0]
    own_blocks = node_ref.shape[1] // tile
    hub_blocks = hub_ref.shape[1] // tile
    farthest = 2**REACH_BITS - 1
    slots = 2 * farthest + 1
    half = hub_half.shape[1]
    piece = half // pieces
    stride = chips // pieces
    shift = parity if stride > 1 else 0
    chunk = tiles // load_sem.shape[0]

    def load(c):
        part = pl.ds(c * chunk, chunk)
        return pltpu.make_async_copy(vals_hbm.at[part], vals.at[part], load_sem.at[c])

    for c in range(load_sem.shape[0]):
        load(c).start()

    barrier = pltpu.get_barrier_semaphore()

    def greet(i, _):
        pl.semaphore_signal(barrier, inc=1, device_id=(lax.rem(me + i, n),), device_id_type=MESH)
        return 0

    lax.fori_loop(1, n, greet, 0)

    for b in range(own_blocks):
        block = node_ref[:, b * tile : (b + 1) * tile]
        cur[b] = block
        node_total[b * width : (b + 1) * width] = block.astype(jnp.float32)
    for b in range(hub_blocks):
        block = hub_ref[:, b * tile : (b + 1) * tile]
        cur[own_blocks + b] = block
        hub_total[b * width : (b + 1) * width] = block.astype(jnp.float32)
    chain[tiles] = jnp.zeros((width, tile), jnp.float32)

    def remote(src, dst, send, recv, target):
        return pltpu.make_async_remote_copy(
            src_ref=src, dst_ref=dst, send_sem=send, recv_sem=recv,
            device_id=(target,), device_id_type=MESH,
        )

    def is_owner():
        return lax.rem(chip, stride) == shift

    my_piece = chip // stride
    my_global = parity * pieces + my_piece

    for layer in range(LAYERS):
        def multiply(g, _):
            base = g * GROUP
            parts = [
                lax.dot_general(
                    cur[col_ref[base + u]], vals[base + u], (((1,), (1,)), ((), ())),
                    preferred_element_type=jnp.float32,
                )
                for u in range(GROUP)
            ]
            for u in range(GROUP):
                chain[base + u] = chain[prev_ref[base + u]] + parts[u]
            return 0

        per = chunk // GROUP
        if layer == 0:
            for c in range(load_sem.shape[0]):
                load(c).wait()
                lax.fori_loop(c * per, (c + 1) * per, multiply, 0)
            pl.semaphore_wait(barrier, n - 1)
        else:
            lax.fori_loop(0, tiles // GROUP, multiply, 0)

        for b in range(hub_blocks):
            hub_own[layer, b * width : (b + 1) * width] = chain[last_ref[slots * own_blocks + b]]
        hub_swap = remote(
            hub_own.at[layer, pl.ds(pl.multiple_of((1 - parity) * half, SUBLANES), half)],
            hub_pair.at[layer], hub_pair_sem.at[layer, 0], hub_pair_sem.at[layer, 1], partner,
        )
        hub_swap.start()

        def gather_slot(slot):
            for b in range(own_blocks):
                own[layer, slot, b * width : (b + 1) * width] = chain[last_ref[slot * own_blocks + b]]

        swaps = []
        for i in range(farthest + 1):
            gather_slot(2 * i)
            swap = remote(
                own.at[layer, 2 * i], pair.at[layer, i],
                pair_send.at[layer, i], pair_recv.at[layer, i], partner,
            )
            swap.start()
            swaps.append(swap)
        for i in range(farthest):
            gather_slot(2 * i + 1)

        hub_swap.wait_recv()
        hub_half[layer] = (
            hub_own[layer, pl.ds(pl.multiple_of(parity * half, SUBLANES), half)] + hub_pair[layer]
        )

        def piece_copy(j):
            owner = j * stride + shift
            place = lax.rem(chip - owner + chips, chips)
            return owner, place, remote(
                hub_half.at[layer, pl.ds(j * piece, piece)],
                hub_got.at[layer, jnp.maximum(place - 1, 0)],
                piece_send.at[layer, j], piece_recv.at[layer], 2 * owner + parity,
            )

        for j in range(pieces):
            owner, place, copy = piece_copy(j)

            @pl.when(owner != chip)
            def _():
                copy.start()

        offsets = [m for m in range(1 - farthest, farthest + 2, 2) if m] + [0]
        sends = []
        for i, m in enumerate(offsets):
            index = (step * (m - 1) + farthest) // 2
            remote(
                own.at[layer, 0], pair.at[layer, index],
                pair_send.at[layer, index], pair_recv.at[layer, index], partner,
            ).wait_recv()
            value = pair[layer, index]
            if m <= farthest:
                value = own[layer, farthest + step * m] + value
            merged[layer, i] = value
            if m:
                copy = remote(
                    merged.at[layer, i], arrived.at[layer, i],
                    node_send.at[layer, i], node_recv.at[layer, i],
                    lax.rem(me + step * m + n, n),
                )
                copy.start()
                sends.append(copy)

        def cast_copy(i):
            rows = pl.ds(pl.multiple_of(my_global * piece, SUBLANES), piece)
            return remote(
                hub_all.at[layer, rows], hub_all.at[layer, rows],
                cast_send.at[layer, i - 1], cast_recv.at[layer, my_global], lax.rem(me + i, n),
            )

        @pl.when(is_owner())
        def _():
            pltpu.make_async_copy(hub_got.at[layer], hub_got.at[layer], piece_recv.at[layer]).wait()
            start = pl.multiple_of(my_piece * piece, SUBLANES)
            total = hub_half[layer, pl.ds(start, piece)]
            for i in range(chips - 1):
                total = total + hub_got[layer, i]
            hub_all[layer, pl.ds(pl.multiple_of(my_global * piece, SUBLANES), piece)] = total

            def cast(i, _):
                cast_copy(i).start()
                return 0

            lax.fori_loop(1, n, cast, 0)

        for copy in sends:
            copy.wait_recv()
        for b in range(own_blocks):
            rows = slice(b * width, (b + 1) * width)
            value = merged[layer, len(offsets) - 1, rows]
            for i in range(len(sends)):
                value = value + arrived[layer, i, rows]
            total = node_total[rows] + value
            if layer < LAYERS - 1:
                cur[b] = value.astype(jnp.bfloat16)
                node_total[rows] = total
            else:
                node_out[:, b * tile : (b + 1) * tile] = total / float(LAYERS + 1)

        def land(g):
            rows = pl.ds(g * piece, piece)
            return remote(
                hub_all.at[layer, rows], hub_all.at[layer, rows],
                cast_send.at[layer, 0], cast_recv.at[layer, g], partner,
            )

        for g in range(2 * pieces):
            @pl.when(jnp.logical_not(jnp.logical_and(is_owner(), my_global == g)))
            def _():
                land(g).wait_recv()

        for b in range(hub_blocks):
            rows = slice(b * width, (b + 1) * width)
            value = hub_all[layer, rows]
            total = hub_total[rows] + value
            if layer < LAYERS - 1:
                cur[own_blocks + b] = value.astype(jnp.bfloat16)
                hub_total[rows] = total
            else:
                hub_out[:, b * tile : (b + 1) * tile] = total / float(LAYERS + 1)

        hub_swap.wait_send()
        for copy in swaps + sends:
            copy.wait_send()
        for j in range(pieces):
            owner, place, copy = piece_copy(j)

            @pl.when(owner != chip)
            def _():
                copy.wait_send()

        @pl.when(is_owner())
        def _():
            def done(i, _):
                cast_copy(i).wait_send()
                return 0

            lax.fori_loop(1, n, done, 0)


def shards(n, node_emb, hub_emb, tile_vals, tile_col, tile_dest):
    tiles, tile, _ = tile_vals.shape
    rows, width = node_emb.shape
    hub_rows = hub_emb.shape[0]
    own_blocks, hub_blocks = rows // tile, hub_rows // tile
    farthest = 2**REACH_BITS - 1
    slots = 2 * farthest + 1
    targets = slots * own_blocks + hub_blocks
    half = hub_blocks * width // 2
    chips = n // 2
    pieces = min(half // SUBLANES, chips)
    order = jnp.arange(tiles, dtype=jnp.int32)
    wanted = jnp.concatenate([tile_dest, jnp.arange(targets, dtype=jnp.int32)])
    limit = jnp.concatenate([order, jnp.full((targets,), tiles, jnp.int32)])
    match = (tile_dest[None, :] == wanted[:, None]) & (order[None, :] < limit[:, None])
    found = jnp.max(jnp.where(match, order[None, :], -1), axis=1)
    found = jnp.where(found < 0, tiles, found)
    block = own_blocks * width
    chunks = CHUNKS if tiles % (CHUNKS * GROUP) == 0 else 1
    f32, dma = jnp.float32, pltpu.SemaphoreType.DMA
    vmem = pl.BlockSpec(memory_space=pltpu.VMEM)
    smem = pl.BlockSpec(memory_space=pltpu.SMEM)
    node_out, hub_out = pl.pallas_call(
        functools.partial(kernel, n, pieces),
        out_shape=(
            jax.ShapeDtypeStruct((width, rows), f32),
            jax.ShapeDtypeStruct((width, hub_rows), f32),
        ),
        in_specs=[pl.BlockSpec(memory_space=pl.ANY), smem, smem, smem, vmem, vmem],
        out_specs=(vmem, vmem),
        scratch_shapes=[
            pltpu.VMEM((tiles, tile, tile), jnp.bfloat16),
            pltpu.VMEM((own_blocks + hub_blocks, width, tile), jnp.bfloat16),
            pltpu.VMEM((tiles + 1, width, tile), f32),
            pltpu.VMEM((LAYERS, slots, block, tile), f32),
            pltpu.VMEM((LAYERS, 2 * half, tile), f32),
            pltpu.VMEM((LAYERS, farthest + 1, block, tile), f32),
            pltpu.VMEM((LAYERS, half, tile), f32),
            pltpu.VMEM((LAYERS, farthest + 1, block, tile), f32),
            pltpu.VMEM((LAYERS, farthest, block, tile), f32),
            pltpu.VMEM((LAYERS, half, tile), f32),
            pltpu.VMEM((LAYERS, chips - 1, half // pieces, tile), f32),
            pltpu.VMEM((LAYERS, 2 * half, tile), f32),
            pltpu.VMEM((block, tile), f32),
            pltpu.VMEM((2 * half, tile), f32),
            dma((chunks,)),
            dma((LAYERS, farthest + 1)),
            dma((LAYERS, farthest + 1)),
            dma((LAYERS, farthest)),
            dma((LAYERS, farthest)),
            dma((LAYERS, 2)),
            dma((LAYERS, pieces)),
            dma((LAYERS,)),
            dma((LAYERS, n - 1)),
            dma((LAYERS, 2 * pieces)),
        ],
        compiler_params=pltpu.CompilerParams(collective_id=0, has_side_effects=True),
    )(tile_vals, tile_col, found[:tiles], found[tiles:], node_emb.T, hub_emb.T)
    return node_out.T, hub_out.T


def solution(mesh):
    in_specs = (P("dom", None), P(), P("dom", None, None), P("dom"), P("dom"))
    out_specs = (P("dom", None), P())
    body = functools.partial(shards, mesh.shape["dom"])
    return jax.shard_map(body, mesh=mesh, in_specs=in_specs, out_specs=out_specs, check_vma=False)
```

time: 342 us -> 50.4 us (0.15)
  waiting for transfers between devices: 258 us -> 0 us
  Pallas kernels: 0 us -> 44.8 us
  matrix products: 23.3 us -> 0 us
  local copies, waits for them, and re-layouts: 24.1 us -> 4.07 us
  starting transfers between devices: 17.9 us -> 0 us
  between operations: 14.2 us -> 0.66 us
    psum x2 -> x0, waiting for transfers between devices: 255 us -> none  [shards(): hub_sum = lax.psum(hub_part, 'dom')]
    pallas_call x0 -> x1, Pallas kernels: none -> 44.8 us  [shards(): pl.pallas_call(functools.partial(kernel, n, pieces), out_shape=(jax.Shape...]
    dot_general x4 -> x0, matrix products: 23.3 us -> none  [the longest x2 14.1 us: shards(): jnp.einsum('tij,tjd->tid', tile_vals, picked, preferred_element_type=jnp....]
    ppermute x12 -> x0, starting transfers between devices: 17.6 us -> none  [shifted(): return lax.ppermute(block, axis, route)]
    dot_general x2 -> x0, local copies, waits for them, and re-layouts: 10.9 us -> none  [shards(): jnp.einsum('tij,tjd->tid', tile_vals, picked, preferred_element_type=jnp....]
    squeeze x14 -> x0, local copies, waits for them, and re-layouts: 7.45 us -> none  [the longest x12 7.08 us: route_partials(): spread[farthest + heading * distance]]
  transfers between devices with their start and end apart: 14 -> 0, of which waited for: 4 -> 0; matrix products, arithmetic and copies ran while one was open for 3% -> 0% of each run, Pallas kernels for 0% -> 0%
where the time goes in v1:
time: 50.4 us; the launch traced here: 51 us
  Pallas kernels  44.8 us (89%)
  local copies, waits for them, and re-layouts  4.07 us (8%)
  other arithmetic  1.54 us (3%)
  between operations  0.66 us (1%)
    pallas_call x1, Pallas kernels, shards(): pl.pallas_call(functools.partial(kernel, n, pieces), out_shape=(jax.Shape...  44.8 us
    unnamed x2, local copies, waits for them, and re-layouts  3.04 us

profile of v1, /device:TPU:0, one launch (start us, length us, event | category | flops | bytes accessed | tf_op | source)
XLA Modules:
  0.0 51.0 jit_solution(7682249852172329625)
XLA Ops:
  0.6 0.7 %pad_add_fusion = s32[158]{0:T(256)S(1)} fusion(s32[30]{0:T(128)S(1)} %iota.7, s32[128]{0:T(128)} %param.9), kind=kLoop, calls=%fused_computation.4 | loop fusion | flops 158 | bytes 1264 | tf_op jit(solution)/shard_map/concatenate | solution.py:258
  1.3 0.9 %select_reduce_fusion = s32[158]{0:T(256)S(1)} fusion(s32[158]{0:T(256)} %constant.1.clone.1, s32[128]{0:T(128)} %param.9, s32[158]{0:T(256)S(1)} %pad_add_fusion), kind=kLoop, calls=%fused_computation | loop fusion | flops 100962 | bytes 2408 | tf_op jit(solution)/shard_map/reduce_max | solution.py:261
  2.2 0.5 %slice.7.last_ref = s32[30]{0:T(128)} slice(s32[158]{0:T(256)S(1)} %compare_select_fusion), slice={[128:158]} | slice | bytes 240 | tf_op jit(solution)/shard_map/slice | solution.py:303
  2.7 0.5 %slice.6.prev_ref = s32[128]{0:T(128)} slice(s32[158]{0:T(256)S(1)} %compare_select_fusion), slice={[0:128]} | slice | bytes 1024 | tf_op jit(solution)/shard_map/slice | solution.py:303
  3.2 44.8 %shard_map.68 = (f32[64,512]{1,0:T(8,128)}, f32[64,256]{1,0:T(8,128)}) custom-call(bf16[128,128,128]{2,1,0:T(8,128)(2,1)} %vals_hbm.1, s32[128]{0:T(128)} %col_ref.1, s32[128]{0:T(128)} %slice.6.prev_ref, s32[30]{0:T(128)} %slice.7.last_ref, bf16[64,512]{1,0:T(8,128)(2,1)} %bitcast.5, bf16[64,256]{1,0:T(8,128)(2,1)} %bitcast.7), custom_call_target="tpu_custom_call" | custom-call | tf_op jit(solution)/shard_map/pallas_call | solution.py:268
  48.0 1.6 %copy.9 = f32[512,64]{0,1:T(8,128)} copy(f32[512,64]{0,1:T(8,128)} %bitcast.4) | data formatting | bytes 262144
  49.5 1.5 %copy.10 = f32[256,64]{0,1:T(8,128)} copy(f32[256,64]{0,1:T(8,128)} %bitcast.6) | data formatting | bytes 131072
  (2 shorter events, 0.0 us)

commit v2 on v1

--- a/solution.py
+++ b/solution.py
@@ -9,23 +9,21 @@
 REACH_BITS = 2
 LAYERS = 2
 CHUNKS = 8
-GROUP = 4
+GROUP = 16
 SUBLANES = 8
 MESH = pl.DeviceIdType.MESH
 
 
 def kernel(
-    n, pieces, vals_hbm, col_ref, prev_ref, last_ref, node_ref, hub_ref,
+    n, pieces, vals_hbm, col_ref, found_ref, node_ref, hub_ref,
     node_out, hub_out,
-    vals, cur, chain, own, hub_own, pair, hub_pair, merged, arrived,
-    hub_half, hub_got, hub_all, node_total, hub_total,
-    load_sem, pair_send, pair_recv, node_send, node_recv, hub_pair_sem,
+    vals, cur, chain, own, hub_own, pair, merged, arrived,
+    hub_got, hub_all, node_total, hub_total,
+    load_sem, pair_send, pair_recv, node_send, node_recv,
     piece_send, piece_recv, cast_send, cast_recv,
 ):
     me = lax.axis_index("dom")
     parity = lax.rem(me, 2)
-    chip = me // 2
-    chips = n // 2
     step = 1 - 2 * parity
     partner = me + step
     tiles, tile, _ = vals.shape
@@ -34,10 +32,8 @@
     hub_blocks = hub_ref.shape[1] // tile
     farthest = 2**REACH_BITS - 1
     slots = 2 * farthest + 1
-    half = hub_half.shape[1]
-    piece = half // pieces
-    stride = chips // pieces
-    shift = parity if stride > 1 else 0
+    piece = hub_own.shape[1] // pieces
+    stride = n // pieces
     chunk = tiles // load_sem.shape[0]
 
     def load(c):
@@ -72,10 +68,9 @@
         )
 
     def is_owner():
-        return lax.rem(chip, stride) == shift
-
-    my_piece = chip // stride
-    my_global = parity * pieces + my_piece
+        return lax.rem(me, stride) == 0
+
+    my_piece = me // stride
 
     for layer in range(LAYERS):
         def multiply(g, _):
@@ -88,7 +83,7 @@
                 for u in range(GROUP)
             ]
             for u in range(GROUP):
-                chain[base + u] = chain[prev_ref[base + u]] + parts[u]
+                chain[base + u] = chain[found_ref[base + u]] + parts[u]
             return 0
 
         per = chunk // GROUP
@@ -101,16 +96,27 @@
             lax.fori_loop(0, tiles // GROUP, multiply, 0)
 
         for b in range(hub_blocks):
-            hub_own[layer, b * width : (b + 1) * width] = chain[last_ref[slots * own_blocks + b]]
-        hub_swap = remote(
-            hub_own.at[layer, pl.ds(pl.multiple_of((1 - parity) * half, SUBLANES), half)],
-            hub_pair.at[layer], hub_pair_sem.at[layer, 0], hub_pair_sem.at[layer, 1], partner,
-        )
-        hub_swap.start()
+            hub_own[layer, b * width : (b + 1) * width] = chain[found_ref[tiles + slots * own_blocks + b]]
+
+        def piece_copy(j):
+            owner = j * stride
+            place = lax.rem(me - owner + n, n)
+            return owner, remote(
+                hub_own.at[layer, pl.ds(j * piece, piece)],
+                hub_got.at[layer, jnp.maximum(place - 1, 0)],
+                piece_send.at[layer, j], piece_recv.at[layer], owner,
+            )
+
+        for j in range(pieces):
+            owner, copy = piece_copy(j)
+
+            @pl.when(owner != me)
+            def _():
+                copy.start()
 
         def gather_slot(slot):
             for b in range(own_blocks):
-                own[layer, slot, b * width : (b + 1) * width] = chain[last_ref[slot * own_blocks + b]]
+                own[layer, slot, b * width : (b + 1) * width] = chain[found_ref[tiles + slot * own_blocks + b]]
 
         swaps = []
         for i in range(farthest + 1):
@@ -123,27 +129,6 @@
             swaps.append(swap)
         for i in range(farthest):
             gather_slot(2 * i + 1)
-
-        hub_swap.wait_recv()
-        hub_half[layer] = (
-            hub_own[layer, pl.ds(pl.multiple_of(parity * half, SUBLANES), half)] + hub_pair[layer]
-        )
-
-        def piece_copy(j):
-            owner = j * stride + shift
-            place = lax.rem(chip - owner + chips, chips)
-            return owner, place, remote(
-                hub_half.at[layer, pl.ds(j * piece, piece)],
-                hub_got.at[layer, jnp.maximum(place - 1, 0)],
-                piece_send.at[layer, j], piece_recv.at[layer], 2 * owner + parity,
-            )
-
-        for j in range(pieces):
-            owner, place, copy = piece_copy(j)
-
-            @pl.when(owner != chip)
-            def _():
-                copy.start()
 
         offsets = [m for m in range(1 - farthest, farthest + 2, 2) if m] + [0]
         sends = []
@@ -167,20 +152,19 @@
                 sends.append(copy)
 
         def cast_copy(i):
-            rows = pl.ds(pl.multiple_of(my_global * piece, SUBLANES), piece)
+            rows = pl.ds(pl.multiple_of(my_piece * piece, SUBLANES), piece)
             return remote(
                 hub_all.at[layer, rows], hub_all.at[layer, rows],
-                cast_send.at[layer, i - 1], cast_recv.at[layer, my_global], lax.rem(me + i, n),
+                cast_send.at[layer, i - 1], cast_recv.at[layer, my_piece], lax.rem(me + i, n),
             )
 
         @pl.when(is_owner())
         def _():
             pltpu.make_async_copy(hub_got.at[layer], hub_got.at[layer], piece_recv.at[layer]).wait()
             start = pl.multiple_of(my_piece * piece, SUBLANES)
-            total = hub_half[layer, pl.ds(start, piece)]
-            for i in range(chips - 1):
-                total = total + hub_got[layer, i]
-            hub_all[layer, pl.ds(pl.multiple_of(my_global * piece, SUBLANES), piece)] = total
+            hub_all[layer, pl.ds(start, piece)] = (
+                hub_own[layer, pl.ds(start, piece)] + jnp.sum(hub_got[layer], axis=0)
+            )
 
             def cast(i, _):
                 cast_copy(i).start()
@@ -209,8 +193,8 @@
                 cast_send.at[layer, 0], cast_recv.at[layer, g], partner,
             )
 
-        for g in range(2 * pieces):
-            @pl.when(jnp.logical_not(jnp.logical_and(is_owner(), my_global == g)))
+        for g in range(pieces):
+            @pl.when(jnp.logical_not(jnp.logical_and(is_owner(), my_piece == g)))
             def _():
                 land(g).wait_recv()
 
@@ -224,13 +208,12 @@
             else:
                 hub_out[:, b * tile : (b + 1) * tile] = total / float(LAYERS + 1)
 
-        hub_swap.wait_send()
         for copy in swaps + sends:
             copy.wait_send()
         for j in range(pieces):
-            owner, place, copy = piece_copy(j)
-
-            @pl.when(owner != chip)
+            owner, copy = piece_copy(j)
+
+            @pl.when(owner != me)
             def _():
                 copy.wait_send()
 
@@ -251,9 +234,8 @@
     farthest = 2**REACH_BITS - 1
     slots = 2 * farthest + 1
     targets = slots * own_blocks + hub_blocks
-    half = hub_blocks * width // 2
-    chips = n // 2
-    pieces = min(half // SUBLANES, chips)
+    packed = hub_blocks * width
+    pieces = min(packed // SUBLANES, n)
     order = jnp.arange(tiles, dtype=jnp.int32)
     wanted = jnp.concatenate([tile_dest, jnp.arange(targets, dtype=jnp.int32)])
     limit = jnp.concatenate([order, jnp.full((targets,), tiles, jnp.int32)])
@@ -271,36 +253,33 @@
             jax.ShapeDtypeStruct((width, rows), f32),
             jax.ShapeDtypeStruct((width, hub_rows), f32),
         ),
-        in_specs=[pl.BlockSpec(memory_space=pl.ANY), smem, smem, smem, vmem, vmem],
+        in_specs=[pl.BlockSpec(memory_space=pl.ANY), smem, smem, vmem, vmem],
         out_specs=(vmem, vmem),
         scratch_shapes=[
             pltpu.VMEM((tiles, tile, tile), jnp.bfloat16),
             pltpu.VMEM((own_blocks + hub_blocks, width, tile), jnp.bfloat16),
             pltpu.VMEM((tiles + 1, width, tile), f32),
             pltpu.VMEM((LAYERS, slots, block, tile), f32),
-            pltpu.VMEM((LAYERS, 2 * half, tile), f32),
+            pltpu.VMEM((LAYERS, packed, tile), f32),
             pltpu.VMEM((LAYERS, farthest + 1, block, tile), f32),
-            pltpu.VMEM((LAYERS, half, tile), f32),
             pltpu.VMEM((LAYERS, farthest + 1, block, tile), f32),
             pltpu.VMEM((LAYERS, farthest, block, tile), f32),
-            pltpu.VMEM((LAYERS, half, tile), f32),
-            pltpu.VMEM((LAYERS, chips - 1, half // pieces, tile), f32),
-            pltpu.VMEM((LAYERS, 2 * half, tile), f32),
+            pltpu.VMEM((LAYERS, n - 1, packed // pieces, tile), f32),
+            pltpu.VMEM((LAYERS, packed, tile), f32),
             pltpu.VMEM((block, tile), f32),
-            pltpu.VMEM((2 * half, tile), f32),
+            pltpu.VMEM((packed, tile), f32),
             dma((chunks,)),
             dma((LAYERS, farthest + 1)),
             dma((LAYERS, farthest + 1)),
             dma((LAYERS, farthest)),
             dma((LAYERS, farthest)),
-            dma((LAYERS, 2)),
             dma((LAYERS, pieces)),
             dma((LAYERS,)),
             dma((LAYERS, n - 1)),
-            dma((LAYERS, 2 * pieces)),
+            dma((LAYERS, pieces)),
         ],
         compiler_params=pltpu.CompilerParams(collective_id=0, has_side_effects=True),
-    )(tile_vals, tile_col, found[:tiles], found[tiles:], node_emb.T, hub_emb.T)
+    )(tile_vals, tile_col, found, node_emb.T, hub_emb.T)
     return node_out.T, hub_out.T
 
 

time: 50.4 us -> 44.2 us (0.88); the launches traced: 51 us -> 43.9 us
  Pallas kernels: 44.8 us -> 38.1 us
  local copies, waits for them, and re-layouts: 4.07 us -> 3.04 us
  other arithmetic: 1.54 us -> 2.1 us
    pallas_call x1, Pallas kernels: 44.8 us -> 38.1 us  [shards(): pl.pallas_call(functools.partial(kernel, n, pieces), out_shape=(jax.Shape...]
    slice x2 -> x0, local copies, waits for them, and re-layouts: 1.03 us -> none  [the longest x1 0.51 us: shards(): found[tiles:]]
    select_n x1, other arithmetic: 0.01 us -> 0.57 us  [shards(): found = jnp.where(found < 0, tiles, found)]
where the time goes in v2:
time: 44.2 us; the launch traced here: 43.9 us
  Pallas kernels  38.1 us (86%)
  local copies, waits for them, and re-layouts  3.04 us (7%)
  other arithmetic  2.1 us (5%)
  between operations  0.65 us (1%)
    pallas_call x1, Pallas kernels, shards(): pl.pallas_call(functools.partial(kernel, n, pieces), out_shape=(jax.Shape...  38.1 us
    unnamed x2, local copies, waits for them, and re-layouts  3.04 us

profile of v2, /device:TPU:0, one launch (start us, length us, event | category | flops | bytes accessed | tf_op | source)
XLA Modules:
  0.0 43.9 jit_solution(14621693423108075860)
XLA Ops:
  0.6 0.7 %pad_add_fusion = s32[158]{0:T(256)S(1)} fusion(s32[30]{0:T(128)S(1)} %iota.7, s32[128]{0:T(128)} %param.9), kind=kLoop, calls=%fused_computation.4 | loop fusion | flops 158 | bytes 1264 | tf_op jit(solution)/shard_map/concatenate | solution.py:240
  1.3 0.9 %select_reduce_fusion = s32[158]{0:T(256)S(1)} fusion(s32[158]{0:T(256)} %constant.1.clone.1, s32[128]{0:T(128)} %param.9, s32[158]{0:T(256)S(1)} %pad_add_fusion), kind=kLoop, calls=%fused_computation | loop fusion | flops 100962 | bytes 2408 | tf_op jit(solution)/shard_map/reduce_max | solution.py:243
  2.2 0.6 %compare_select_fusion.found_ref = s32[158]{0:T(256)} fusion(s32[158]{0:T(256)S(1)} %select_reduce_fusion), kind=kLoop, calls=%fused_computation.3 | loop fusion | flops 316 | bytes 1264 | tf_op jit(solution)/shard_map/jit(_where)/select_n | solution.py:244
  2.7 38.1 %shard_map.68 = (f32[64,512]{1,0:T(8,128)}, f32[64,256]{1,0:T(8,128)}) custom-call(bf16[128,128,128]{2,1,0:T(8,128)(2,1)} %vals_hbm.1, s32[128]{0:T(128)} %col_ref.1, s32[158]{0:T(256)} %compare_select_fusion.found_ref, bf16[64,512]{1,0:T(8,128)(2,1)} %bitcast.5, bf16[64,256]{1,0:T(8,128)(2,1)} %bitcast.7), custom_call_target="tpu_custom_call" | custom-call | tf_op jit(solution)/shard_map/pallas_call | solution.py:250
  40.8 1.6 %copy.9 = f32[512,64]{0,1:T(8,128)} copy(f32[512,64]{0,1:T(8,128)} %bitcast.4) | data formatting | bytes 262144
  42.4 1.5 %copy.10 = f32[256,64]{0,1:T(8,128)} copy(f32[256,64]{0,1:T(8,128)} %bitcast.6) | data formatting | bytes 131072
  (1 shorter events, 0.0 us)

commit v3 on v2

--- a/solution.py
+++ b/solution.py
@@ -8,18 +8,18 @@
 
 REACH_BITS = 2
 LAYERS = 2
-CHUNKS = 8
-GROUP = 16
+CHUNKS = 4
+GROUP = 32
 SUBLANES = 8
 MESH = pl.DeviceIdType.MESH
 
 
 def kernel(
-    n, pieces, vals_hbm, col_ref, found_ref, node_ref, hub_ref,
+    n, pieces, vals_hbm, col_ref, dest_ref, node_ref, hub_ref,
     node_out, hub_out,
-    vals, cur, chain, own, hub_own, pair, merged, arrived,
+    vals, cur, chain, table, found_ref, own, hub_own, pair, merged, arrived,
     hub_got, hub_all, node_total, hub_total,
-    load_sem, pair_send, pair_recv, node_send, node_recv,
+    load_sem, table_sem, pair_send, pair_recv, node_send, node_recv,
     piece_send, piece_recv, cast_send, cast_recv,
 ):
     me = lax.axis_index("dom")
@@ -51,6 +51,17 @@
 
     lax.fori_loop(1, n, greet, 0)
 
+    across = jnp.broadcast_to(dest_ref[...], (tiles, tiles))
+    down = across.T
+    order = lax.broadcasted_iota(jnp.int32, (tiles, tiles), 0)
+    place = lax.broadcasted_iota(jnp.int32, (tiles, tiles), 1)
+    earlier = jnp.logical_and(down == across, order < place)
+    for i, match in enumerate((earlier, down == place)):
+        found = jnp.max(jnp.where(match, order, -1), axis=0, keepdims=True)
+        table[i : i + 1] = jnp.where(found < 0, tiles, found)
+    table_copy = pltpu.make_async_copy(table, found_ref, table_sem)
+    table_copy.start()
+
     for b in range(own_blocks):
         block = node_ref[:, b * tile : (b + 1) * tile]
         cur[b] = block
@@ -60,6 +71,7 @@
         cur[own_blocks + b] = block
         hub_total[b * width : (b + 1) * width] = block.astype(jnp.float32)
     chain[tiles] = jnp.zeros((width, tile), jnp.float32)
+    table_copy.wait()
 
     def remote(src, dst, send, recv, target):
         return pltpu.make_async_remote_copy(
@@ -83,7 +95,7 @@
                 for u in range(GROUP)
             ]
             for u in range(GROUP):
-                chain[base + u] = chain[found_ref[base + u]] + parts[u]
+                chain[base + u] = chain[found_ref[0, base + u]] + parts[u]
             return 0
 
         per = chunk // GROUP
@@ -96,7 +108,7 @@
             lax.fori_loop(0, tiles // GROUP, multiply, 0)
 
         for b in range(hub_blocks):
-            hub_own[layer, b * width : (b + 1) * width] = chain[found_ref[tiles + slots * own_blocks + b]]
+            hub_own[layer, b * width : (b + 1) * width] = chain[found_ref[1, slots * own_blocks + b]]
 
         def piece_copy(j):
             owner = j * stride
@@ -116,7 +128,7 @@
 
         def gather_slot(slot):
             for b in range(own_blocks):
-                own[layer, slot, b * width : (b + 1) * width] = chain[found_ref[tiles + slot * own_blocks + b]]
+                own[layer, slot, b * width : (b + 1) * width] = chain[found_ref[1, slot * own_blocks + b]]
 
         swaps = []
         for i in range(farthest + 1):
@@ -233,15 +245,8 @@
     own_blocks, hub_blocks = rows // tile, hub_rows // tile
     farthest = 2**REACH_BITS - 1
     slots = 2 * farthest + 1
-    targets = slots * own_blocks + hub_blocks
     packed = hub_blocks * width
     pieces = min(packed // SUBLANES, n)
-    order = jnp.arange(tiles, dtype=jnp.int32)
-    wanted = jnp.concatenate([tile_dest, jnp.arange(targets, dtype=jnp.int32)])
-    limit = jnp.concatenate([order, jnp.full((targets,), tiles, jnp.int32)])
-    match = (tile_dest[None, :] == wanted[:, None]) & (order[None, :] < limit[:, None])
-    found = jnp.max(jnp.where(match, order[None, :], -1), axis=1)
-    found = jnp.where(found < 0, tiles, found)
     block = own_blocks * width
     chunks = CHUNKS if tiles % (CHUNKS * GROUP) == 0 else 1
     f32, dma = jnp.float32, pltpu.SemaphoreType.DMA
@@ -253,12 +258,14 @@
             jax.ShapeDtypeStruct((width, rows), f32),
             jax.ShapeDtypeStruct((width, hub_rows), f32),
         ),
-        in_specs=[pl.BlockSpec(memory_space=pl.ANY), smem, smem, vmem, vmem],
+        in_specs=[pl.BlockSpec(memory_space=pl.ANY), smem, vmem, vmem, vmem],
         out_specs=(vmem, vmem),
         scratch_shapes=[
             pltpu.VMEM((tiles, tile, tile), jnp.bfloat16),
             pltpu.VMEM((own_blocks + hub_blocks, width, tile), jnp.bfloat16),
             pltpu.VMEM((tiles + 1, width, tile), f32),
+            pltpu.VMEM((2, tiles), jnp.int32),
+            pltpu.SMEM((2, tiles), jnp.int32),
             pltpu.VMEM((LAYERS, slots, block, tile), f32),
             pltpu.VMEM((LAYERS, packed, tile), f32),
             pltpu.VMEM((LAYERS, farthest + 1, block, tile), f32),
@@ -269,6 +276,7 @@
             pltpu.VMEM((block, tile), f32),
             pltpu.VMEM((packed, tile), f32),
             dma((chunks,)),
+            dma,
             dma((LAYERS, farthest + 1)),
             dma((LAYERS, farthest + 1)),
             dma((LAYERS, farthest)),
@@ -279,7 +287,7 @@
             dma((LAYERS, pieces)),
         ],
         compiler_params=pltpu.CompilerParams(collective_id=0, has_side_effects=True),
-    )(tile_vals, tile_col, found, node_emb.T, hub_emb.T)
+    )(tile_vals, tile_col, tile_dest.reshape(1, tiles), node_emb.T, hub_emb.T)
     return node_out.T, hub_out.T
 
 

time: 44.2 us -> 41.1 us (0.930)
  other arithmetic: 2.1 us -> 0 us
  Pallas kernels: 38.1 us -> 37.2 us
    pallas_call x1, Pallas kernels: 38.1 us -> 37.2 us  [shards(): pl.pallas_call(functools.partial(kernel, n, pieces), out_shape=(jax.Shape...]
    reduce_max x1 -> x0, other arithmetic: 0.87 us -> none  [shards(): found = jnp.max(jnp.where(match, order[None, :], -1), axis=1)]
    concatenate x1 -> x0, other arithmetic: 0.66 us -> none  [shards(): wanted = jnp.concatenate([tile_dest, jnp.arange(targets, dtype=jnp.int32)])]
    select_n x1 -> x0, other arithmetic: 0.57 us -> none  [shards(): found = jnp.where(found < 0, tiles, found)]
where the time goes in v3:
time: 41.1 us; the launch traced here: 40.9 us
  Pallas kernels  37.2 us (91%)
  local copies, waits for them, and re-layouts  3.04 us (7%)
  between operations  0.64 us (2%)
    pallas_call x1, Pallas kernels, shards(): pl.pallas_call(functools.partial(kernel, n, pieces), out_shape=(jax.Shape...  37.2 us
    unnamed x2, local copies, waits for them, and re-layouts  3.04 us

profile of v3, /device:TPU:0, one launch (start us, length us, event | category | flops | bytes accessed | tf_op | source)
XLA Modules:
  0.0 40.9 jit_solution(8740541234095555904)
XLA Ops:
  0.6 37.2 %shard_map.68 = (f32[64,512]{1,0:T(8,128)}, f32[64,256]{1,0:T(8,128)}) custom-call(bf16[128,128,128]{2,1,0:T(8,128)(2,1)} %vals_hbm.1, s32[128]{0:T(128)} %col_ref.1, s32[1,128]{1,0:T(1,128)} %bitcast.9, bf16[64,512]{1,0:T(8,128)(2,1)} %bitcast.6, bf16[64,256]{1,0:T(8,128)(2,1)} %bitcast.8), custom_call_target="tpu_custom_call" | custom-call | tf_op jit(solution)/shard_map/pallas_call | solution.py:255
  37.8 1.6 %copy.9 = f32[512,64]{0,1:T(8,128)} copy(f32[512,64]{0,1:T(8,128)} %bitcast.5) | data formatting | bytes 262144
  39.4 1.5 %copy.10 = f32[256,64]{0,1:T(8,128)} copy(f32[256,64]{0,1:T(8,128)} %bitcast.7) | data formatting | bytes 131072

commit v4 on v3

--- a/solution.py
+++ b/solution.py
@@ -286,7 +286,7 @@
             dma((LAYERS, n - 1)),
             dma((LAYERS, pieces)),
         ],
-        compiler_params=pltpu.CompilerParams(collective_id=0, has_side_effects=True),
+        compiler_params=pltpu.CompilerParams(collective_id=0, has_side_effects=True, vmem_limit_bytes=52 * 2**20),
     )(tile_vals, tile_col, tile_dest.reshape(1, tiles), node_emb.T, hub_emb.T)
     return node_out.T, hub_out.T
 

time: 41.1 us -> 41.3 us (level)
  local copies, waits for them, and re-layouts: 3.04 us -> 4.19 us
  Pallas kernels: 37.2 us -> 36.3 us
    unnamed x2 -> x10, local copies, waits for them, and re-layouts: 3.04 us -> 4.19 us
    pallas_call x1, Pallas kernels: 37.2 us -> 36.3 us  [shards(): pl.pallas_call(functools.partial(kernel, n, pieces), out_shape=(jax.Shape...]
where the time goes in v4:
time: 41.3 us; the launch traced here: 41.1 us
  Pallas kernels  36.3 us (88%)
  local copies, waits for them, and re-layouts  4.19 us (10%)
  between operations  0.65 us (2%)
    pallas_call x1, Pallas kernels, shards(): pl.pallas_call(functools.partial(kernel, n, pieces), out_shape=(jax.Shape...  36.3 us
    unnamed x10, local copies, waits for them, and re-layouts  4.19 us

profile of v4, /device:TPU:0, one launch (start us, length us, event | category | flops | bytes accessed | tf_op | source)
XLA Modules:
  0.0 41.1 jit_solution(17279425447630615163)
XLA Ops:
  0.6 0.0 copy-start
  0.6 0.8 %copy-done = bf16[512,64]{0,1:T(8,128)(2,1)S(1)} copy-done((bf16[512,64]{0,1:T(8,128)(2,1)S(1)}, bf16[512,64]{0,1:T(8,128)(2,1)}, u32[]{:S(2)}) %copy-start) | copy-done | bytes 65560
  1.5 0.0 copy-start.1
  1.5 0.8 %copy-done.1 = bf16[256,64]{0,1:T(8,128)(2,1)S(1)} copy-done((bf16[256,64]{0,1:T(8,128)(2,1)S(1)}, bf16[256,64]{0,1:T(8,128)(2,1)}, u32[]{:S(2)}) %copy-start.1) | copy-done | bytes 32792
  2.2 0.0 copy-start.2
  2.2 0.7 %copy-done.2 = s32[128]{0:T(128)S(1)} copy-done((s32[128]{0:T(128)S(1)}, s32[128]{0:T(128)}, u32[]{:S(2)}) %copy-start.2) | copy-done | bytes 536
  2.9 0.0 copy-start.3
  2.9 0.7 %copy-done.3 = s32[128]{0:T(128)S(1)} copy-done((s32[128]{0:T(128)S(1)}, s32[128]{0:T(128)}, u32[]{:S(2)}) %copy-start.3) | copy-done | bytes 536
  3.5 36.3 %shard_map.68 = (f32[64,512]{1,0:T(8,128)S(1)}, f32[64,256]{1,0:T(8,128)S(1)}) custom-call(bf16[128,128,128]{2,1,0:T(8,128)(2,1)} %vals_hbm.1, s32[128]{0:T(128)S(1)} %copy-done.2, s32[1,128]{1,0:T(1,128)S(1)} %bitcast.9, bf16[64,512]{1,0:T(8,128)(2,1)S(1)} %bitcast.6, bf16[64,256]{1,0:T(8,128)(2,1)S(1)} %bitcast.8), custom_call_target="tpu_custom_call" | custom-call | tf_op jit(solution)/shard_map/pallas_call | solution.py:255
  39.9 0.7 %copy.9 = f32[512,64]{0,1:T(8,128)} copy(f32[512,64]{0,1:T(8,128)S(1)} %bitcast.5) | data formatting | bytes 262144
  40.5 0.6 %copy.10 = f32[256,64]{0,1:T(8,128)} copy(f32[256,64]{0,1:T(8,128)S(1)} %bitcast.7) | data formatting | bytes 131072
Async XLA Ops:
  0.6 0.8 %copy-start = (bf16[512,64]{0,1:T(8,128)(2,1)S(1)}, bf16[512,64]{0,1:T(8,128)(2,1)}, u32[]{:S(2)}) copy-start(bf16[512,64]{0,1:T(8,128)(2,1)} %param.5) | copy-start | bytes 196612
  1.5 0.8 %copy-start.1 = (bf16[256,64]{0,1:T(8,128)(2,1)S(1)}, bf16[256,64]{0,1:T(8,128)(2,1)}, u32[]{:S(2)}) copy-start(bf16[256,64]{0,1:T(8,128)(2,1)} %param.6) | copy-start | bytes 98308
  2.2 0.7 %copy-start.2 = (s32[128]{0:T(128)S(1)}, s32[128]{0:T(128)}, u32[]{:S(2)}) copy-start(s32[128]{0:T(128)} %col_ref.1) | copy-start | bytes 1540
  2.9 0.7 %copy-start.3 = (s32[128]{0:T(128)S(1)}, s32[128]{0:T(128)}, u32[]{:S(2)}) copy-start(s32[128]{0:T(128)} %param.9) | copy-start | bytes 1540

commit v5 on v3

--- a/solution.py
+++ b/solution.py
@@ -130,8 +130,11 @@
             for b in range(own_blocks):
                 own[layer, slot, b * width : (b + 1) * width] = chain[found_ref[1, slot * own_blocks + b]]
 
+        offsets = [m for m in range(1 - farthest, farthest + 2, 2) if m] + [0]
         swaps = []
-        for i in range(farthest + 1):
+        for m in offsets:
+            first = (m - 1 + farthest) // 2
+            i = parity * first + (1 - parity) * (farthest - first)
             gather_slot(2 * i)
             swap = remote(
                 own.at[layer, 2 * i], pair.at[layer, i],
@@ -142,7 +145,6 @@
         for i in range(farthest):
             gather_slot(2 * i + 1)
 
-        offsets = [m for m in range(1 - farthest, farthest + 2, 2) if m] + [0]
         sends = []
         for i, m in enumerate(offsets):
             index = (step * (m - 1) + farthest) // 2

time: 41.1 us -> 40.6 us (0.988)
  Pallas kernels: 37.2 us -> 36.6 us
    pallas_call x1, Pallas kernels: 37.2 us -> 36.6 us  [shards(): pl.pallas_call(functools.partial(kernel, n, pieces), out_shape=(jax.Shape...]
where the time goes in v5:
time: 40.6 us; the launch traced here: 40.3 us
  Pallas kernels  36.6 us (90%)
  local copies, waits for them, and re-layouts  3.04 us (7%)
  between operations  0.64 us (2%)
    pallas_call x1, Pallas kernels, shards(): pl.pallas_call(functools.partial(kernel, n, pieces), out_shape=(jax.Shape...  36.6 us
    unnamed x2, local copies, waits for them, and re-layouts  3.04 us

profile of v5, /device:TPU:0, one launch (start us, length us, event | category | flops | bytes accessed | tf_op | source)
XLA Modules:
  0.0 40.3 jit_solution(1017430349737440144)
XLA Ops:
  0.6 36.6 %shard_map.68 = (f32[64,512]{1,0:T(8,128)}, f32[64,256]{1,0:T(8,128)}) custom-call(bf16[128,128,128]{2,1,0:T(8,128)(2,1)} %vals_hbm.1, s32[128]{0:T(128)} %col_ref.1, s32[1,128]{1,0:T(1,128)} %bitcast.9, bf16[64,512]{1,0:T(8,128)(2,1)} %bitcast.6, bf16[64,256]{1,0:T(8,128)(2,1)} %bitcast.8), custom_call_target="tpu_custom_call" | custom-call | tf_op jit(solution)/shard_map/pallas_call | solution.py:257
  37.3 1.6 %copy.9 = f32[512,64]{0,1:T(8,128)} copy(f32[512,64]{0,1:T(8,128)} %bitcast.5) | data formatting | bytes 262144
  38.8 1.5 %copy.10 = f32[256,64]{0,1:T(8,128)} copy(f32[256,64]{0,1:T(8,128)} %bitcast.7) | data formatting | bytes 131072
